TPU v7x, 32 devices: a whole 2x2x4 slice. The times are simulated.
32 devices in a mesh: vp: 8 (over z, y), rep: 4 (over x, core).
Axes of the slice: x: 2, y: 2, z: 4, core: 2. Of those that a mesh axis runs over, the one named last changes fastest.
Arguments:
- features: bfloat16 [65536, 256], P(('vp', 'rep')), may hold values from -48 to 48
- tile_values: bfloat16 [8192, 128, 128], P(('vp', 'rep')), may hold values from 0 to 0.0014648438
- tile_cols: int32 [8192], P(('vp', 'rep')), may hold values from 0 to 31, as said below
- halo_rows: int32 [32, 4, 4], P(('vp', 'rep')), may hold values from 0 to 15
Outputs:
- scores: bfloat16 [65536, 256], P(('vp', 'rep'))
Inputs may be any that keep to these rules, and one draw needn't show every extreme that they name: `tile_cols`: values below 16 name one of the shard's own row blocks; value 16 + o * 4 + j names the j-th block sent by peer o. Every value occurs on every shard.
All inputs are finite; a program needn't handle non-finite values.
Results may differ from a plain program's by a relative error of at most 0.002.
Values may be sent and summed in bfloat16 or wider, within the bound.
A program may use at most 128 MiB of HBM per device.

v0:
```python
import functools

import jax
import jax.numpy as jnp
from jax import lax
from jax.experimental import pallas as pl
from jax.experimental.pallas import tpu as pltpu
from jax.sharding import PartitionSpec as P

ITERS = 3
LANES = 128
MESH = pl.DeviceIdType.MESH
LOADS = 8
UNROLL = 64


def kernel(vp_count, rep_count, vertices, slots, halves, *refs):
    cols_ref, rows_ref, feat_hbm, tiles_hbm, out_hbm = refs[:5]
    it_refs = iter(refs[5:])
    take = lambda count: [next(it_refs) for _ in range(count)]
    tiles = take(1)[0]
    tables = [take(halves) for _ in range(ITERS)]
    feats = take(halves)
    owns = take(halves)
    sends = [take(halves) for _ in range(ITERS)]
    finals = take(halves)
    stages = take(halves)
    mine = [take(halves) for _ in range(ITERS)]
    got = [take(halves) for _ in range(ITERS)]
    order, place = take(2)
    (tile_sem, feat_sem, table_sem, out_sem, send_sem, recv_sem, mass_send, mass_recv) = take(8)

    nblocks, tile_size = feats[0].shape[0], feats[0].shape[1]
    ntiles = tiles.shape[0]
    per_row = ntiles // nblocks
    my_vp, my_rep = lax.axis_index("vp"), lax.axis_index("rep")
    me = my_vp * rep_count + my_rep
    shards = vp_count * rep_count

    own_loads, table_loads = [], []
    for h in range(halves):
        part = feat_hbm.at[:, :, pl.ds(h * LANES, LANES)]
        own_loads.append(pltpu.make_async_copy(part, feats[h], feat_sem.at[h]))
        table_loads.append(
            pltpu.make_async_copy(part, tables[0][h].at[pl.ds(0, nblocks)], table_sem.at[h])
        )
    for h in range(halves):
        own_loads[h].start()
    for h in range(halves):
        table_loads[h].start()
    chunk = ntiles // LOADS
    tile_loads = []
    for k in range(LOADS):
        piece = pl.ds(k * chunk, chunk)
        tile_loads.append(pltpu.make_async_copy(tiles_hbm.at[piece], tiles.at[piece], tile_sem.at[k]))
        tile_loads[-1].start()

    def device_at(distance):
        flat = lax.rem(me + distance + shards, shards)
        return flat // rep_count, lax.rem(flat, rep_count)

    def peer_at(o):
        size = 1 + 3 * (o // 2)
        return device_at(size * (1 - 2 * lax.rem(o, 2)))

    barrier = pltpu.get_barrier_semaphore()

    def greet(k, carry):
        pl.semaphore_signal(barrier, inc=1, device_id=device_at(k), device_id_type=MESH)
        return carry

    lax.fori_loop(1, shards, greet, 0)

    def sent(o, j):
        return rows_ref[0, o, j]

    turns = []
    for b in range(nblocks):
        turn = jnp.int32(4)
        for g in reversed(range(4)):
            hit = sent((g + 2) % 4, 0) == b
            for j in range(1, slots):
                hit = hit | (sent((g + 2) % 4, j) == b)
            turn = jnp.where(hit, g, turn)
        turns.append(turn * nblocks + b)
    places = []
    for b in range(nblocks):
        at = jnp.int32(0)
        for c in range(nblocks):
            if c != b:
                at = at + jnp.where(turns[c] < turns[b], 1, 0)
        places.append(at)
        place[b] = at
    for b in range(4 * slots):
        place[nblocks + b] = jnp.int32(nblocks + b)
    for k in range(nblocks):
        row = jnp.int32(0)
        for b in range(nblocks):
            row = row + jnp.where(places[b] == k, b, 0)
        order[k] = row

    pl.semaphore_wait(barrier, shards - 1)

    def halo_copy(it, h, o):
        at = (it * halves + h) * 4 + o
        return pltpu.make_async_remote_copy(
            src_ref=sends[it][h].at[pl.ds(o * slots, slots)],
            dst_ref=tables[it][h].at[pl.ds(nblocks + o * slots, slots)],
            send_sem=send_sem.at[at],
            recv_sem=recv_sem.at[at],
            device_id=peer_at(o),
            device_id_type=MESH,
        )

    def send_halo(it, h, o, source):
        for j in range(slots):
            row = rows_ref[0, o, j]
            sends[it][h][o * slots + j] = source[place[row] if it else row]
        halo_copy(it, h, o).start()

    def mass_copy(it, h, k):
        at = it * halves + h
        return pltpu.make_async_remote_copy(
            src_ref=mine[it][h],
            dst_ref=got[it][h].at[k - 1],
            send_sem=mass_send.at[at, k - 1],
            recv_sem=mass_recv.at[at, k - 1],
            device_id=device_at(k),
            device_id_type=MESH,
        )

    def each_other(it, h, act):
        def one(k, carry):
            act(mass_copy(it, h, k))
            return carry

        lax.fori_loop(1, shards, one, 0, unroll=shards <= UNROLL)

    def mass_first(it, h, mass):
        mine[it][h][...] = mass
        each_other(it, h, lambda copy: copy.start())

    def mass_total(it, h):
        each_other(it, h, lambda copy: copy.wait_recv())
        total = mine[it][h][...] + jnp.sum(got[it][h][...], axis=0)
        return 1.0 / jnp.sqrt(0.05 + total / vertices)

    def propagate(it, h, gain):
        table = tables[it][h]
        last = it + 1 == ITERS

        def row(k, mass):
            r = k if last else order[k]
            first = r * per_row
            slot = lambda t: cols_ref[first + t]
            source = slot if it == 0 else lambda t: place[slot(t)]
            left = jnp.concatenate([tiles[first + t] for t in range(per_row)], axis=1)
            right = jnp.concatenate([table[source(t)] for t in range(per_row)], axis=0)
            total = jnp.dot(left, right, preferred_element_type=jnp.float32)
            blended = gain * total + 0.1 * feats[h][r].astype(jnp.float32)
            if last:
                finals[h][k] = blended
            else:
                rounded = blended.astype(jnp.bfloat16)
                owns[h][k] = rounded
                tables[it + 1][h][k] = rounded
            squares = (blended * blended).reshape(tile_size // 8, 8, LANES)
            return mass + jnp.sum(squares, axis=0)

        def group(g, mass):
            for k in range(nblocks // 4):
                mass = row(g * (nblocks // 4) + k, mass)
            if not last:
                send_halo(it + 1, h, lax.rem(g + 2, 4), owns[h])
            return mass

        mass = lax.fori_loop(0, 4, group, jnp.zeros((8, LANES), jnp.float32))
        return jnp.sum(mass, axis=0, keepdims=True)

    for h in range(halves):
        own_loads[h].wait()
        for o in (2, 3, 0, 1):
            send_halo(0, h, o, feats[h])
    for h in range(halves):
        table_loads[h].wait()
    for load in tile_loads:
        load.wait()

    def finish(h):
        scale = mass_total(ITERS - 1, h)
        for b in range(nblocks):
            stages[h][b] = (finals[h][b] * scale).astype(jnp.bfloat16)
        pltpu.make_async_copy(
            stages[h], out_hbm.at[:, :, pl.ds(h * LANES, LANES)], out_sem.at[h]
        ).start()

    for it in range(ITERS):
        for h in range(halves):
            for o in range(4):
                halo_copy(it, h, o).wait_recv()
            gain = 0.9 if it == 0 else 0.9 * mass_total(it - 1, h)
            mass = propagate(it, h, gain)
            mass_first(it, h, mass)
    for h in range(halves):
        finish(h)
    for it in range(ITERS):
        for h in range(halves):
            for o in range(4):
                halo_copy(it, h, o).wait_send()
            each_other(it, h, lambda copy: copy.wait_send())
    for h in range(halves):
        pltpu.make_async_copy(
            stages[h], out_hbm.at[:, :, pl.ds(h * LANES, LANES)], out_sem.at[h]
        ).wait()


def local(vp_count, rep_count, features, tile_values, tile_cols, halo_rows):
    tile_size = tile_values.shape[1]
    rows, classes = features.shape
    nblocks = rows // tile_size
    slots = halo_rows.shape[2]
    halves = classes // LANES
    shards = vp_count * rep_count
    block = (tile_size, LANES)
    bf16, f32 = jnp.bfloat16, jnp.float32
    each = ITERS * halves
    scratch = [pltpu.VMEM(tile_values.shape, bf16)]
    scratch += [pltpu.VMEM((nblocks + 4 * slots,) + block, bf16)] * each
    scratch += [pltpu.VMEM((nblocks,) + block, bf16)] * (2 * halves)
    scratch += [pltpu.VMEM((4 * slots,) + block, bf16)] * each
    scratch += [pltpu.VMEM((nblocks,) + block, f32)] * halves
    scratch += [pltpu.VMEM((nblocks,) + block, bf16)] * halves
    scratch += [pltpu.VMEM((1, LANES), f32)] * each
    scratch += [pltpu.VMEM((shards - 1, 1, LANES), f32)] * each
    scratch += [pltpu.SMEM((nblocks,), jnp.int32), pltpu.SMEM((nblocks + 4 * slots,), jnp.int32)]
    dma = lambda *shape: pltpu.SemaphoreType.DMA(shape)
    scratch += [dma(LOADS), dma(halves), dma(halves), dma(halves), dma(each * 4), dma(each * 4)]
    scratch += [dma(each, shards - 1)] * 2
    out = pl.pallas_call(
        functools.partial(kernel, vp_count, rep_count, rows * shards, slots, halves),
        out_shape=jax.ShapeDtypeStruct((nblocks, tile_size, classes), bf16),
        in_specs=[pl.BlockSpec(memory_space=pltpu.SMEM)] * 2
        + [pl.BlockSpec(memory_space=pl.ANY)] * 2,
        out_specs=pl.BlockSpec(memory_space=pl.ANY),
        scratch_shapes=scratch,
        compiler_params=pltpu.CompilerParams(
            collective_id=0, has_side_effects=True, vmem_limit_bytes=60 * 1024 * 1024
        ),
    )(tile_cols, halo_rows, features.reshape(nblocks, tile_size, classes), tile_values)
    return out.reshape(rows, classes)


def solution(mesh):
    return jax.shard_map(
        functools.partial(local, mesh.shape["vp"], mesh.shape["rep"]),
        mesh=mesh,
        in_specs=(
            P(("vp", "rep"), None),
            P(("vp", "rep"), None, None),
            P(("vp", "rep")),
            P(("vp", "rep"), None, None),
        ),
        out_specs=P(("vp", "rep"), None),
        check_vma=False,
    )
```

profile of v0, /device:TPU:0, one launch (start us, length us, event | category | flops | bytes accessed | tf_op | source)
XLA Modules:
  0.0 69.0 jit_solution(8555206069593556239)
XLA Ops:
  0.0 66.8 %shard_map.46 = bf16[16,128,256]{2,1,0:T(8,128)(2,1)} custom-call(s32[256]{0:T(256)} %refs_0_.1, s32[1,4,4]{2,1,0:T(4,128)} %refs_1_.1, bf16[16,128,256]{2,1,0:T(8,128)(2,1)} %bitcast.3, bf16[256,128,128]{2,1,0:T(8,128)(2,1)} %refs_3_.1), custom_call_target="tpu_custom_call" | custom-call | tf_op jit(solution)/shard_map/pallas_call | solution.py:239
  66.8 2.3 %copy.6 = bf16[2048,256]{1,0:T(8,128)(2,1)} copy(bf16[2048,256]{1,0:T(8,128)(2,1)} %bitcast.2) | data formatting | bytes 2097152
where the time goes:
time: 69.2 us; the launch traced here: 69 us
  Pallas kernels  66.8 us (97%)
  local copies, waits for them, and re-layouts  2.26 us (3%)
    pallas_call x1, Pallas kernels, local(): pl.pallas_call(functools.partial(kernel, vp_count, rep_count, rows * shar...  66.8 us
    unnamed x1, local copies, waits for them, and re-layouts  2.26 us

commit v1 on v0

--- a/solution.py
+++ b/solution.py
@@ -123,25 +123,34 @@
         return pltpu.make_async_remote_copy(
             src_ref=mine[it][h],
             dst_ref=got[it][h].at[k - 1],
-            send_sem=mass_send.at[at, k - 1],
-            recv_sem=mass_recv.at[at, k - 1],
+            send_sem=mass_send.at[at],
+            recv_sem=mass_recv.at[at],
             device_id=device_at(k),
             device_id_type=MESH,
         )
 
-    def each_other(it, h, act):
-        def one(k, carry):
-            act(mass_copy(it, h, k))
-            return carry
-
-        lax.fori_loop(1, shards, one, 0, unroll=shards <= UNROLL)
+    def mass_all(it, h):
+        at = it * halves + h
+        return pltpu.make_async_remote_copy(
+            src_ref=got[it][h],
+            dst_ref=got[it][h],
+            send_sem=mass_send.at[at],
+            recv_sem=mass_recv.at[at],
+            device_id=device_at(1),
+            device_id_type=MESH,
+        )
 
     def mass_first(it, h, mass):
         mine[it][h][...] = mass
-        each_other(it, h, lambda copy: copy.start())
+
+        def one(k, carry):
+            mass_copy(it, h, k).start()
+            return carry
+
+        lax.fori_loop(1, shards, one, 0, unroll=shards <= UNROLL)
 
     def mass_total(it, h):
-        each_other(it, h, lambda copy: copy.wait_recv())
+        mass_all(it, h).wait_recv()
         total = mine[it][h][...] + jnp.sum(got[it][h][...], axis=0)
         return 1.0 / jnp.sqrt(0.05 + total / vertices)
 
@@ -207,7 +216,7 @@
         for h in range(halves):
             for o in range(4):
                 halo_copy(it, h, o).wait_send()
-            each_other(it, h, lambda copy: copy.wait_send())
+            mass_all(it, h).wait_send()
     for h in range(halves):
         pltpu.make_async_copy(
             stages[h], out_hbm.at[:, :, pl.ds(h * LANES, LANES)], out_sem.at[h]
@@ -235,7 +244,7 @@
     scratch += [pltpu.SMEM((nblocks,), jnp.int32), pltpu.SMEM((nblocks + 4 * slots,), jnp.int32)]
     dma = lambda *shape: pltpu.SemaphoreType.DMA(shape)
     scratch += [dma(LOADS), dma(halves), dma(halves), dma(halves), dma(each * 4), dma(each * 4)]
-    scratch += [dma(each, shards - 1)] * 2
+    scratch += [dma(each)] * 2
     out = pl.pallas_call(
         functools.partial(kernel, vp_count, rep_count, rows * shards, slots, halves),
         out_shape=jax.ShapeDtypeStruct((nblocks, tile_size, classes), bf16),

time: 69.2 us -> 65.9 us (0.952)
  Pallas kernels: 66.8 us -> 63.5 us
    pallas_call x1, Pallas kernels: 66.8 us -> 63.5 us  [local(): pl.pallas_call(functools.partial(kernel, vp_count, rep_count, rows * shar...]
where the time goes in v1:
time: 65.9 us; the launch traced here: 65.7 us
  Pallas kernels  63.5 us (96%)
  local copies, waits for them, and re-layouts  2.26 us (3%)
    pallas_call x1, Pallas kernels, local(): pl.pallas_call(functools.partial(kernel, vp_count, rep_count, rows * shar...  63.5 us
    unnamed x1, local copies, waits for them, and re-layouts  2.26 us

profile of v1, /device:TPU:0, one launch (start us, length us, event | category | flops | bytes accessed | tf_op | source)
XLA Modules:
  0.0 65.7 jit_solution(8736088471873904742)
XLA Ops:
  0.0 63.5 %shard_map.46 = bf16[16,128,256]{2,1,0:T(8,128)(2,1)} custom-call(s32[256]{0:T(256)} %refs_0_.1, s32[1,4,4]{2,1,0:T(4,128)} %refs_1_.1, bf16[16,128,256]{2,1,0:T(8,128)(2,1)} %bitcast.3, bf16[256,128,128]{2,1,0:T(8,128)(2,1)} %refs_3_.1), custom_call_target="tpu_custom_call" | custom-call | tf_op jit(solution)/shard_map/pallas_call | solution.py:248
  63.5 2.3 %copy.6 = bf16[2048,256]{1,0:T(8,128)(2,1)} copy(bf16[2048,256]{1,0:T(8,128)(2,1)} %bitcast.2) | data formatting | bytes 2097152

commit v2 on v1

--- a/solution.py
+++ b/solution.py
@@ -12,23 +12,22 @@
 MESH = pl.DeviceIdType.MESH
 LOADS = 8
 UNROLL = 64
+VMEM_LIMIT = 40 * 1024 * 1024
 
 
 def kernel(vp_count, rep_count, vertices, slots, halves, *refs):
-    cols_ref, rows_ref, feat_hbm, tiles_hbm, out_hbm = refs[:5]
-    it_refs = iter(refs[5:])
+    cols_hbm, rows_hbm, feat_hbm, tiles_hbm, finals_ref, scale_ref = refs[:6]
+    it_refs = iter(refs[6:])
     take = lambda count: [next(it_refs) for _ in range(count)]
     tiles = take(1)[0]
     tables = [take(halves) for _ in range(ITERS)]
     feats = take(halves)
     owns = take(halves)
     sends = [take(halves) for _ in range(ITERS)]
-    finals = take(halves)
-    stages = take(halves)
     mine = [take(halves) for _ in range(ITERS)]
     got = [take(halves) for _ in range(ITERS)]
-    order, place = take(2)
-    (tile_sem, feat_sem, table_sem, out_sem, send_sem, recv_sem, mass_send, mass_recv) = take(8)
+    order, place, cols_ref, rows_ref = take(4)
+    (index_sem, tile_sem, feat_sem, table_sem, send_sem, recv_sem, mass_send, mass_recv) = take(8)
 
     nblocks, tile_size = feats[0].shape[0], feats[0].shape[1]
     ntiles = tiles.shape[0]
@@ -37,6 +36,10 @@
     me = my_vp * rep_count + my_rep
     shards = vp_count * rep_count
 
+    cols_load = pltpu.make_async_copy(cols_hbm, cols_ref, index_sem.at[0])
+    rows_load = pltpu.make_async_copy(rows_hbm, rows_ref, index_sem.at[1])
+    rows_load.start()
+    cols_load.start()
     own_loads, table_loads = [], []
     for h in range(halves):
         part = feat_hbm.at[:, :, pl.ds(h * LANES, LANES)]
@@ -70,6 +73,9 @@
         return carry
 
     lax.fori_loop(1, shards, greet, 0)
+
+    rows_load.wait()
+    cols_load.wait()
 
     def sent(o, j):
         return rows_ref[0, o, j]
@@ -168,7 +174,7 @@
             total = jnp.dot(left, right, preferred_element_type=jnp.float32)
             blended = gain * total + 0.1 * feats[h][r].astype(jnp.float32)
             if last:
-                finals[h][k] = blended
+                finals_ref[k, :, h * LANES:(h + 1) * LANES] = blended
             else:
                 rounded = blended.astype(jnp.bfloat16)
                 owns[h][k] = rounded
@@ -196,12 +202,7 @@
         load.wait()
 
     def finish(h):
-        scale = mass_total(ITERS - 1, h)
-        for b in range(nblocks):
-            stages[h][b] = (finals[h][b] * scale).astype(jnp.bfloat16)
-        pltpu.make_async_copy(
-            stages[h], out_hbm.at[:, :, pl.ds(h * LANES, LANES)], out_sem.at[h]
-        ).start()
+        scale_ref[:, h * LANES:(h + 1) * LANES] = mass_total(ITERS - 1, h)
 
     for it in range(ITERS):
         for h in range(halves):
@@ -217,10 +218,6 @@
             for o in range(4):
                 halo_copy(it, h, o).wait_send()
             mass_all(it, h).wait_send()
-    for h in range(halves):
-        pltpu.make_async_copy(
-            stages[h], out_hbm.at[:, :, pl.ds(h * LANES, LANES)], out_sem.at[h]
-        ).wait()
 
 
 def local(vp_count, rep_count, features, tile_values, tile_cols, halo_rows):
@@ -237,26 +234,28 @@
     scratch += [pltpu.VMEM((nblocks + 4 * slots,) + block, bf16)] * each
     scratch += [pltpu.VMEM((nblocks,) + block, bf16)] * (2 * halves)
     scratch += [pltpu.VMEM((4 * slots,) + block, bf16)] * each
-    scratch += [pltpu.VMEM((nblocks,) + block, f32)] * halves
-    scratch += [pltpu.VMEM((nblocks,) + block, bf16)] * halves
     scratch += [pltpu.VMEM((1, LANES), f32)] * each
     scratch += [pltpu.VMEM((shards - 1, 1, LANES), f32)] * each
     scratch += [pltpu.SMEM((nblocks,), jnp.int32), pltpu.SMEM((nblocks + 4 * slots,), jnp.int32)]
+    scratch += [pltpu.SMEM(tile_cols.shape, jnp.int32), pltpu.SMEM(halo_rows.shape, jnp.int32)]
     dma = lambda *shape: pltpu.SemaphoreType.DMA(shape)
-    scratch += [dma(LOADS), dma(halves), dma(halves), dma(halves), dma(each * 4), dma(each * 4)]
+    scratch += [dma(2), dma(LOADS), dma(halves), dma(halves), dma(each * 4), dma(each * 4)]
     scratch += [dma(each)] * 2
-    out = pl.pallas_call(
+    operands = (tile_cols, halo_rows, features.reshape(nblocks, tile_size, classes), tile_values)
+    finals, scale = pl.pallas_call(
         functools.partial(kernel, vp_count, rep_count, rows * shards, slots, halves),
-        out_shape=jax.ShapeDtypeStruct((nblocks, tile_size, classes), bf16),
-        in_specs=[pl.BlockSpec(memory_space=pltpu.SMEM)] * 2
-        + [pl.BlockSpec(memory_space=pl.ANY)] * 2,
-        out_specs=pl.BlockSpec(memory_space=pl.ANY),
+        out_shape=(
+            pltpu.VMEM((nblocks, tile_size, classes), f32),
+            pltpu.VMEM((1, classes), f32),
+        ),
+        in_specs=[pl.BlockSpec(memory_space=pltpu.HBM)] * 4,
+        out_specs=(pl.BlockSpec(memory_space=pltpu.VMEM),) * 2,
         scratch_shapes=scratch,
         compiler_params=pltpu.CompilerParams(
-            collective_id=0, has_side_effects=True, vmem_limit_bytes=60 * 1024 * 1024
+            collective_id=0, has_side_effects=True, vmem_limit_bytes=VMEM_LIMIT
         ),
-    )(tile_cols, halo_rows, features.reshape(nblocks, tile_size, classes), tile_values)
-    return out.reshape(rows, classes)
+    )(*[pltpu.with_memory_space_constraint(x, pltpu.HBM) for x in operands])
+    return (finals * scale[None]).astype(bf16).reshape(rows, classes)
 
 
 def solution(mesh):

time: 65.9 us -> 63.2 us (0.959)
  local copies, waits for them, and re-layouts: 2.26 us -> 0 us
  Pallas kernels: 63.5 us -> 61.9 us
  other arithmetic: 0 us -> 1.18 us
    unnamed x1 -> x0, local copies, waits for them, and re-layouts: 2.26 us -> none
    pallas_call x1, Pallas kernels: 63.5 us -> 61.9 us  [local(): pl.pallas_call(functools.partial(kernel, vp_count, rep_count, rows * shar...]
    convert_element_type x0 -> x1, other arithmetic: none -> 1.18 us  [local(): return (finals * scale[None]).astype(bf16).reshape(rows, classes)]
where the time goes in v2:
time: 63.2 us; the launch traced here: 63.1 us
  Pallas kernels  61.9 us (98%)
  other arithmetic  1.18 us (2%)
    pallas_call x1, Pallas kernels, local(): pl.pallas_call(functools.partial(kernel, vp_count, rep_count, rows * shar...  61.9 us

profile of v2, /device:TPU:0, one launch (start us, length us, event | category | flops | bytes accessed | tf_op | source)
XLA Modules:
  0.0 63.1 jit_solution(11703079539658203237)
XLA Ops:
  0.0 61.9 %shard_map.46 = (f32[16,128,256]{2,1,0:T(8,128)S(1)}, f32[1,256]{1,0:T(1,128)S(1)}) custom-call(s32[256]{0:T(256)} %refs_0_.1, s32[1,4,4]{2,1,0:T(4,128)} %refs_1_.1, bf16[16,128,256]{2,1,0:T(8,128)(2,1)} %bitcast.4, bf16[256,128,128]{2,1,0:T(8,128)(2,1)} %refs_3_.1), custom_call_target="tpu_custom_call" | custom-call | tf_op jit(solution)/shard_map/pallas_call | solution.py:245
  61.9 1.2 %multiply_convert_fusion = bf16[16,128,256]{2,1,0:T(8,128)(2,1)} fusion(f32[16,128,256]{2,1,0:T(8,128)S(1)} %get-tuple-element.7, f32[256]{0:T(256)S(1)} %bitcast.3), kind=kLoop, calls=%fused_computation | loop fusion | flops 1048576 | bytes 3146752 | tf_op jit(solution)/shard_map/convert_element_type | solution.py:258

commit v3 on v2

--- a/solution.py
+++ b/solution.py
@@ -24,10 +24,13 @@
     feats = take(halves)
     owns = take(halves)
     sends = [take(halves) for _ in range(ITERS)]
-    mine = [take(halves) for _ in range(ITERS)]
-    got = [take(halves) for _ in range(ITERS)]
+    first = take(halves)
+    second = take(halves)
+    mine = take(ITERS)
+    got = take(ITERS)
+    relays = take(ITERS * halves - 1)
     order, place, cols_ref, rows_ref = take(4)
-    (index_sem, tile_sem, feat_sem, table_sem, send_sem, recv_sem, mass_send, mass_recv) = take(8)
+    (index_sem, tile_sem, feat_sem, table_sem, send_sem, recv_sem, mass_send, mass_recv, relay_send, relay_recv) = take(10)
 
     nblocks, tile_size = feats[0].shape[0], feats[0].shape[1]
     ntiles = tiles.shape[0]
@@ -80,13 +83,17 @@
     def sent(o, j):
         return rows_ref[0, o, j]
 
+    direct = 2 + lax.rem(me // 4, 2)
+    passed = 5 - direct
+    peers = (passed, direct, 0, 1)
+
     turns = []
     for b in range(nblocks):
         turn = jnp.int32(4)
         for g in reversed(range(4)):
-            hit = sent((g + 2) % 4, 0) == b
+            hit = sent(peers[g], 0) == b
             for j in range(1, slots):
-                hit = hit | (sent((g + 2) % 4, j) == b)
+                hit = hit | (sent(peers[g], j) == b)
             turn = jnp.where(hit, g, turn)
         turns.append(turn * nblocks + b)
     places = []
@@ -118,106 +125,195 @@
             device_id_type=MESH,
         )
 
-    def send_halo(it, h, o, source):
+    def fill_halo(it, h, o, source):
         for j in range(slots):
             row = rows_ref[0, o, j]
             sends[it][h][o * slots + j] = source[place[row] if it else row]
-        halo_copy(it, h, o).start()
-
-    def mass_copy(it, h, k):
+
+    steps = [(it, h) for it in range(ITERS) for h in range(halves)]
+
+    def relay_copy(it, h):
         at = it * halves + h
         return pltpu.make_async_remote_copy(
-            src_ref=mine[it][h],
-            dst_ref=got[it][h].at[k - 1],
-            send_sem=mass_send.at[at],
-            recv_sem=mass_recv.at[at],
+            src_ref=sends[it][h].at[pl.ds(passed * slots, slots)],
+            dst_ref=relays[at - 1],
+            send_sem=relay_send.at[at - 1],
+            recv_sem=relay_recv.at[at - 1],
+            device_id=device_at(8 * (5 - 2 * passed)),
+            device_id_type=MESH,
+        )
+
+    def forward_copy(it, h):
+        at = it * halves + h
+        return pltpu.make_async_remote_copy(
+            src_ref=relays[at - 1],
+            dst_ref=tables[it][h].at[pl.ds(nblocks + passed * slots, slots)],
+            send_sem=send_sem.at[at * 4 + passed],
+            recv_sem=recv_sem.at[at * 4 + passed],
+            device_id=peer_at(direct),
+            device_id_type=MESH,
+        )
+
+    def mass_copy(it, k):
+        return pltpu.make_async_remote_copy(
+            src_ref=mine[it],
+            dst_ref=got[it].at[k - 1],
+            send_sem=mass_send.at[it],
+            recv_sem=mass_recv.at[it],
             device_id=device_at(k),
             device_id_type=MESH,
         )
 
-    def mass_all(it, h):
-        at = it * halves + h
-        return pltpu.make_async_remote_copy(
-            src_ref=got[it][h],
-            dst_ref=got[it][h],
-            send_sem=mass_send.at[at],
-            recv_sem=mass_recv.at[at],
+    def mass_all(it):
+        return pltpu.make_async_remote_copy(
+            src_ref=got[it],
+            dst_ref=got[it],
+            send_sem=mass_send.at[it],
+            recv_sem=mass_recv.at[it],
             device_id=device_at(1),
             device_id_type=MESH,
         )
 
-    def mass_first(it, h, mass):
-        mine[it][h][...] = mass
+    def mass_first(it, masses):
+        mine[it][...] = jnp.concatenate(masses, axis=1)
 
         def one(k, carry):
-            mass_copy(it, h, k).start()
+            mass_copy(it, k).start()
             return carry
 
         lax.fori_loop(1, shards, one, 0, unroll=shards <= UNROLL)
 
-    def mass_total(it, h):
-        mass_all(it, h).wait_recv()
-        total = mine[it][h][...] + jnp.sum(got[it][h][...], axis=0)
+    def mass_total(it):
+        mass_all(it).wait_recv()
+        total = mine[it][...] + jnp.sum(got[it][...], axis=0)
         return 1.0 / jnp.sqrt(0.05 + total / vertices)
 
-    def propagate(it, h, gain):
+    def half_of(gain, h):
+        return gain[:, h * LANES : (h + 1) * LANES]
+
+    def squares(blended):
+        return jnp.sum((blended * blended).reshape(tile_size // 8, 8, LANES), axis=0)
+
+    def propagate(it, h, gains=None):
         table = tables[it][h]
         last = it + 1 == ITERS
 
         def row(k, mass):
             r = k if last else order[k]
-            first = r * per_row
-            slot = lambda t: cols_ref[first + t]
+            first_tile = r * per_row
+            slot = lambda t: cols_ref[first_tile + t]
             source = slot if it == 0 else lambda t: place[slot(t)]
-            left = jnp.concatenate([tiles[first + t] for t in range(per_row)], axis=1)
+            left = jnp.concatenate([tiles[first_tile + t] for t in range(per_row)], axis=1)
             right = jnp.concatenate([table[source(t)] for t in range(per_row)], axis=0)
             total = jnp.dot(left, right, preferred_element_type=jnp.float32)
-            blended = gain * total + 0.1 * feats[h][r].astype(jnp.float32)
             if last:
-                finals_ref[k, :, h * LANES:(h + 1) * LANES] = blended
-            else:
-                rounded = blended.astype(jnp.bfloat16)
-                owns[h][k] = rounded
-                tables[it + 1][h][k] = rounded
-            squares = (blended * blended).reshape(tile_size // 8, 8, LANES)
-            return mass + jnp.sum(squares, axis=0)
+                inner = 0.729 * gains[0] * total + first[h][place[r]]
+                if len(gains) == 1:
+                    finals_ref[k, :, h * LANES : (h + 1) * LANES] = inner
+                    return mass
+                blended = gains[1] * inner + 0.1 * feats[h][r].astype(jnp.float32)
+                finals_ref[k, :, h * LANES : (h + 1) * LANES] = blended
+                return mass + squares(blended)
+            rounded = total.astype(jnp.bfloat16)
+            owns[h][k] = rounded
+            tables[it + 1][h][k] = rounded
+            if it:
+                second[h][k] = total
+                return mass
+            first[h][k] = total
+            return mass + squares(0.9 * total + 0.1 * feats[h][r].astype(jnp.float32))
 
         def group(g, mass):
             for k in range(nblocks // 4):
                 mass = row(g * (nblocks // 4) + k, mass)
             if not last:
-                send_halo(it + 1, h, lax.rem(g + 2, 4), owns[h])
+                o = jnp.where(g == 0, passed, jnp.where(g == 1, direct, g - 2))
+                fill_halo(it + 1, h, o, owns[h])
+
+                @pl.when(g == 0)
+                def _():
+                    relay_copy(it + 1, h).start()
+
+                @pl.when(g > 0)
+                def _():
+                    halo_copy(it + 1, h, o).start()
+
             return mass
 
         mass = lax.fori_loop(0, 4, group, jnp.zeros((8, LANES), jnp.float32))
         return jnp.sum(mass, axis=0, keepdims=True)
 
+    def blend_second(h, g1):
+        def row(k, mass):
+            one, two = first[h][k], second[h][k]
+            feat = feats[h][order[k]].astype(jnp.float32)
+            first[h][k] = 0.09 * (0.9 * g1 * two + one)
+            return mass + squares(0.9 * g1 * (0.9 * two + 0.1 * one) + 0.1 * feat)
+
+        mass = lax.fori_loop(0, nblocks, row, jnp.zeros((8, LANES), jnp.float32), unroll=4)
+        return jnp.sum(mass, axis=0, keepdims=True)
+
+    def blend_third(h, g2):
+        def row(k, mass):
+            inner = finals_ref[k, :, h * LANES : (h + 1) * LANES]
+            blended = g2 * inner + 0.1 * feats[h][k].astype(jnp.float32)
+            finals_ref[k, :, h * LANES : (h + 1) * LANES] = blended
+            return mass + squares(blended)
+
+        mass = lax.fori_loop(0, nblocks, row, jnp.zeros((8, LANES), jnp.float32), unroll=4)
+        return jnp.sum(mass, axis=0, keepdims=True)
+
     for h in range(halves):
         own_loads[h].wait()
-        for o in (2, 3, 0, 1):
-            send_halo(0, h, o, feats[h])
+        for o in peers:
+            fill_halo(0, h, o, feats[h])
+        if h:
+            relay_copy(0, h).start()
+        for o in peers[1:] if h else peers:
+            halo_copy(0, h, o).start()
     for h in range(halves):
         table_loads[h].wait()
     for load in tile_loads:
         load.wait()
 
-    def finish(h):
-        scale_ref[:, h * LANES:(h + 1) * LANES] = mass_total(ITERS - 1, h)
-
+    def halos(it, h):
+        for o in range(4):
+            halo_copy(it, h, o).wait_recv()
+
+    masses, g1 = [], None
+    for at, (it, h) in enumerate(steps):
+        if at + 1 < len(steps):
+            relay_copy(*steps[at + 1]).wait_recv()
+            forward_copy(*steps[at + 1]).start()
+        halos(it, h)
+        final = h + 1 == halves
+        if it == 0:
+            masses.append(propagate(0, h))
+        elif it == 1:
+            propagate(1, h)
+        elif not final:
+            propagate(2, h, (half_of(g1, h),))
+        else:
+            g2 = mass_total(1)
+            masses = [blend_third(other, half_of(g2, other)) for other in range(h)]
+            masses.append(propagate(2, h, (half_of(g1, h), half_of(g2, h))))
+        if it == 0 and final:
+            mass_first(0, masses)
+        if it == 1 and final:
+            g1 = mass_total(0)
+            mass_first(1, [blend_second(each, half_of(g1, each)) for each in range(halves)])
+    for at, step in enumerate(steps):
+        for o in peers[1:]:
+            halo_copy(*step, o).wait_send()
+        if at:
+            relay_copy(*step).wait_send()
+            forward_copy(*step).wait_send()
+        else:
+            halo_copy(*step, passed).wait_send()
+    mass_first(2, masses)
+    scale_ref[...] = mass_total(2)
     for it in range(ITERS):
-        for h in range(halves):
-            for o in range(4):
-                halo_copy(it, h, o).wait_recv()
-            gain = 0.9 if it == 0 else 0.9 * mass_total(it - 1, h)
-            mass = propagate(it, h, gain)
-            mass_first(it, h, mass)
-    for h in range(halves):
-        finish(h)
-    for it in range(ITERS):
-        for h in range(halves):
-            for o in range(4):
-                halo_copy(it, h, o).wait_send()
-            mass_all(it, h).wait_send()
+        mass_all(it).wait_send()
 
 
 def local(vp_count, rep_count, features, tile_values, tile_cols, halo_rows):
@@ -234,13 +330,16 @@
     scratch += [pltpu.VMEM((nblocks + 4 * slots,) + block, bf16)] * each
     scratch += [pltpu.VMEM((nblocks,) + block, bf16)] * (2 * halves)
     scratch += [pltpu.VMEM((4 * slots,) + block, bf16)] * each
-    scratch += [pltpu.VMEM((1, LANES), f32)] * each
-    scratch += [pltpu.VMEM((shards - 1, 1, LANES), f32)] * each
+    scratch += [pltpu.VMEM((nblocks,) + block, f32)] * (2 * halves)
+    scratch += [pltpu.VMEM((1, classes), f32)] * ITERS
+    scratch += [pltpu.VMEM((shards - 1, 1, classes), f32)] * ITERS
+    scratch += [pltpu.VMEM((slots,) + block, bf16)] * (each - 1)
     scratch += [pltpu.SMEM((nblocks,), jnp.int32), pltpu.SMEM((nblocks + 4 * slots,), jnp.int32)]
     scratch += [pltpu.SMEM(tile_cols.shape, jnp.int32), pltpu.SMEM(halo_rows.shape, jnp.int32)]
     dma = lambda *shape: pltpu.SemaphoreType.DMA(shape)
     scratch += [dma(2), dma(LOADS), dma(halves), dma(halves), dma(each * 4), dma(each * 4)]
-    scratch += [dma(each)] * 2
+    scratch += [dma(ITERS)] * 2
+    scratch += [dma(each - 1)] * 2
     operands = (tile_cols, halo_rows, features.reshape(nblocks, tile_size, classes), tile_values)
     finals, scale = pl.pallas_call(
         functools.partial(kernel, vp_count, rep_count, rows * shards, slots, halves),

time: 63.2 us -> 60.9 us (0.964)
  Pallas kernels: 61.9 us -> 59.5 us
    pallas_call x1, Pallas kernels: 61.9 us -> 59.5 us  [local(): pl.pallas_call(functools.partial(kernel, vp_count, rep_count, rows * shar...]
where the time goes in v3:
time: 60.9 us; the launch traced here: 60.7 us
  Pallas kernels  59.5 us (98%)
  other arithmetic  1.18 us (2%)
    pallas_call x1, Pallas kernels, local(): pl.pallas_call(functools.partial(kernel, vp_count, rep_count, rows * shar...  59.5 us

profile of v3, /device:TPU:0, one launch (start us, length us, event | category | flops | bytes accessed | tf_op | source)
XLA Modules:
  0.0 60.7 jit_solution(7421236273172378401)
XLA Ops:
  0.0 59.5 %shard_map.46 = (f32[16,128,256]{2,1,0:T(8,128)S(1)}, f32[1,256]{1,0:T(1,128)S(1)}) custom-call(s32[256]{0:T(256)} %refs_0_.1, s32[1,4,4]{2,1,0:T(4,128)} %refs_1_.1, bf16[16,128,256]{2,1,0:T(8,128)(2,1)} %bitcast.4, bf16[256,128,128]{2,1,0:T(8,128)(2,1)} %refs_3_.1), custom_call_target="tpu_custom_call" | custom-call | tf_op jit(solution)/shard_map/pallas_call | solution.py:344
  59.5 1.2 %multiply_convert_fusion = bf16[16,128,256]{2,1,0:T(8,128)(2,1)} fusion(f32[16,128,256]{2,1,0:T(8,128)S(1)} %get-tuple-element.7, f32[256]{0:T(256)S(1)} %bitcast.3), kind=kLoop, calls=%fused_computation | loop fusion | flops 1048576 | bytes 3146752 | tf_op jit(solution)/shard_map/convert_element_type | solution.py:357

commit v4 on v3

--- a/solution.py
+++ b/solution.py
@@ -11,6 +11,7 @@
 LANES = 128
 MESH = pl.DeviceIdType.MESH
 LOADS = 8
+LATE = 4
 UNROLL = 64
 VMEM_LIMIT = 40 * 1024 * 1024
 
@@ -29,6 +30,7 @@
     mine = take(ITERS)
     got = take(ITERS)
     relays = take(ITERS * halves - 1)
+    late, dense = take(2)
     order, place, cols_ref, rows_ref = take(4)
     (index_sem, tile_sem, feat_sem, table_sem, send_sem, recv_sem, mass_send, mass_recv, relay_send, relay_recv) = take(10)
 
@@ -145,9 +147,10 @@
 
     def forward_copy(it, h):
         at = it * halves + h
+        table = tables[it][h].at[pl.ds(nblocks + passed * slots, slots)]
         return pltpu.make_async_remote_copy(
             src_ref=relays[at - 1],
-            dst_ref=tables[it][h].at[pl.ds(nblocks + passed * slots, slots)],
+            dst_ref=late if at + 1 == len(steps) else table,
             send_sem=send_sem.at[at * 4 + passed],
             recv_sem=recv_sem.at[at * 4 + passed],
             device_id=peer_at(direct),
@@ -194,7 +197,7 @@
     def squares(blended):
         return jnp.sum((blended * blended).reshape(tile_size // 8, 8, LANES), axis=0)
 
-    def propagate(it, h, gains=None):
+    def propagate(it, h, g1=None, g2=None):
         table = tables[it][h]
         last = it + 1 == ITERS
 
@@ -207,13 +210,13 @@
             right = jnp.concatenate([table[source(t)] for t in range(per_row)], axis=0)
             total = jnp.dot(left, right, preferred_element_type=jnp.float32)
             if last:
-                inner = 0.729 * gains[0] * total + first[h][place[r]]
-                if len(gains) == 1:
-                    finals_ref[k, :, h * LANES : (h + 1) * LANES] = inner
+                finals_ref[k, :, h * LANES : (h + 1) * LANES] = 0.729 * g1 * total + first[h][place[r]]
+                if g2 is None:
                     return mass
-                blended = gains[1] * inner + 0.1 * feats[h][r].astype(jnp.float32)
-                finals_ref[k, :, h * LANES : (h + 1) * LANES] = blended
-                return mass + squares(blended)
+                return tuple(
+                    part + squares(blend_third(other, k, half_of(g2, other), 0.0))
+                    for other, part in enumerate(mass)
+                )
             rounded = total.astype(jnp.bfloat16)
             owns[h][k] = rounded
             tables[it + 1][h][k] = rounded
@@ -240,8 +243,9 @@
 
             return mass
 
-        mass = lax.fori_loop(0, 4, group, jnp.zeros((8, LANES), jnp.float32))
-        return jnp.sum(mass, axis=0, keepdims=True)
+        none = jnp.zeros((8, LANES), jnp.float32)
+        mass = lax.fori_loop(0, 4, group, none if g2 is None else (none,) * h, unroll=4)
+        return jax.tree.map(lambda part: jnp.sum(part, axis=0, keepdims=True), mass)
 
     def blend_second(h, g1):
         def row(k, mass):
@@ -253,14 +257,53 @@
         mass = lax.fori_loop(0, nblocks, row, jnp.zeros((8, LANES), jnp.float32), unroll=4)
         return jnp.sum(mass, axis=0, keepdims=True)
 
-    def blend_third(h, g2):
-        def row(k, mass):
-            inner = finals_ref[k, :, h * LANES : (h + 1) * LANES]
-            blended = g2 * inner + 0.1 * feats[h][k].astype(jnp.float32)
-            finals_ref[k, :, h * LANES : (h + 1) * LANES] = blended
-            return mass + squares(blended)
-
-        mass = lax.fori_loop(0, nblocks, row, jnp.zeros((8, LANES), jnp.float32), unroll=4)
+    def blend_third(h, k, g2, more):
+        inner = finals_ref[k, :, h * LANES : (h + 1) * LANES] + more
+        blended = g2 * inner + 0.1 * feats[h][k].astype(jnp.float32)
+        finals_ref[k, :, h * LANES : (h + 1) * LANES] = blended
+        return blended
+
+    def gather_late():
+        part = tile_size // 4
+
+        def row(r, carry):
+            for p in range(4):
+                sums = [jnp.zeros((part, tile_size), jnp.float32)] * slots
+                for t in range(per_row):
+                    tile = tiles[r * per_row + t, p * part : (p + 1) * part].astype(jnp.float32)
+                    slot = cols_ref[r * per_row + t] - nblocks - direct * slots
+                    sums = [total + jnp.where(slot == j, tile, 0.0) for j, total in enumerate(sums)]
+                for j, total in enumerate(sums):
+                    columns = slice(j * tile_size, (j + 1) * tile_size)
+                    dense[r, p * part : (p + 1) * part, columns] = total.astype(jnp.bfloat16)
+            return carry
+
+        lax.fori_loop(0, nblocks, row, 0)
+
+    def late_wait():
+        at = len(steps) - 1
+        pltpu.make_async_remote_copy(
+            src_ref=late,
+            dst_ref=late,
+            send_sem=send_sem.at[at * 4 + direct],
+            recv_sem=recv_sem.at[at * 4 + direct],
+            device_id=peer_at(direct),
+            device_id_type=MESH,
+        ).wait_recv()
+
+    def propagate_late(h, g1, g2):
+        right = late[...].reshape(slots * tile_size, LANES)
+        count = nblocks // LATE
+
+        def group(g, mass):
+            left = dense[pl.ds(g * count, count)].reshape(count * tile_size, slots * tile_size)
+            total = jnp.dot(left, right, preferred_element_type=jnp.float32)
+            for k in range(count):
+                more = 0.729 * g1 * total[k * tile_size : (k + 1) * tile_size]
+                mass = mass + squares(blend_third(h, g * count + k, g2, more))
+            return mass
+
+        mass = lax.fori_loop(0, LATE, group, jnp.zeros((8, LANES), jnp.float32), unroll=LATE)
         return jnp.sum(mass, axis=0, keepdims=True)
 
     for h in range(halves):
@@ -275,11 +318,14 @@
         table_loads[h].wait()
     for load in tile_loads:
         load.wait()
+    tables[-1][-1][pl.ds(nblocks + direct * slots, slots)] = jnp.zeros(late.shape, jnp.bfloat16)
 
     def halos(it, h):
-        for o in range(4):
-            halo_copy(it, h, o).wait_recv()
-
+        for o in (0, 1, passed, direct):
+            if o is not direct or (it, h) != steps[-1]:
+                halo_copy(it, h, o).wait_recv()
+
+    gather_late()
     masses, g1 = [], None
     for at, (it, h) in enumerate(steps):
         if at + 1 < len(steps):
@@ -292,11 +338,12 @@
         elif it == 1:
             propagate(1, h)
         elif not final:
-            propagate(2, h, (half_of(g1, h),))
+            propagate(2, h, half_of(g1, h))
         else:
             g2 = mass_total(1)
-            masses = [blend_third(other, half_of(g2, other)) for other in range(h)]
-            masses.append(propagate(2, h, (half_of(g1, h), half_of(g2, h))))
+            masses = list(propagate(2, h, half_of(g1, h), g2))
+            late_wait()
+            masses.append(propagate_late(h, half_of(g1, h), half_of(g2, h)))
         if it == 0 and final:
             mass_first(0, masses)
         if it == 1 and final:
@@ -333,7 +380,8 @@
     scratch += [pltpu.VMEM((nblocks,) + block, f32)] * (2 * halves)
     scratch += [pltpu.VMEM((1, classes), f32)] * ITERS
     scratch += [pltpu.VMEM((shards - 1, 1, classes), f32)] * ITERS
-    scratch += [pltpu.VMEM((slots,) + block, bf16)] * (each - 1)
+    scratch += [pltpu.VMEM((slots,) + block, bf16)] * each
+    scratch += [pltpu.VMEM((nblocks, tile_size, slots * tile_size), bf16)]
     scratch += [pltpu.SMEM((nblocks,), jnp.int32), pltpu.SMEM((nblocks + 4 * slots,), jnp.int32)]
     scratch += [pltpu.SMEM(tile_cols.shape, jnp.int32), pltpu.SMEM(halo_rows.shape, jnp.int32)]
     dma = lambda *shape: pltpu.SemaphoreType.DMA(shape)

time: 60.9 us -> 59 us (0.969)
  Pallas kernels: 59.5 us -> 57.7 us
    pallas_call x1, Pallas kernels: 59.5 us -> 57.7 us  [local(): pl.pallas_call(functools.partial(kernel, vp_count, rep_count, rows * shar...]
where the time goes in v4:
time: 59 us; the launch traced here: 58.9 us
  Pallas kernels  57.7 us (98%)
  other arithmetic  1.18 us (2%)
    pallas_call x1, Pallas kernels, local(): pl.pallas_call(functools.partial(kernel, vp_count, rep_count, rows * shar...  57.7 us
    convert_element_type x1, other arithmetic, local(): return (finals * scale[None]).astype(bf16).reshape(rows, classes)  1.18 us

profile of v4, /device:TPU:0, one launch (start us, length us, event | category | flops | bytes accessed | tf_op | source)
XLA Modules:
  0.0 58.9 jit_solution(11230160542279233246)
XLA Ops:
  0.0 57.7 %shard_map.46 = (f32[16,128,256]{2,1,0:T(8,128)S(1)}, f32[1,256]{1,0:T(1,128)S(1)}) custom-call(s32[256]{0:T(256)} %refs_0_.1, s32[1,4,4]{2,1,0:T(4,128)} %refs_1_.1, bf16[16,128,256]{2,1,0:T(8,128)(2,1)} %bitcast.4, bf16[256,128,128]{2,1,0:T(8,128)(2,1)} %refs_3_.1), custom_call_target="tpu_custom_call" | custom-call | tf_op jit(solution)/shard_map/pallas_call | solution.py:392
  57.7 1.2 %multiply_convert_fusion = bf16[16,128,256]{2,1,0:T(8,128)(2,1)} fusion(f32[16,128,256]{2,1,0:T(8,128)S(1)} %get-tuple-element.7, f32[256]{0:T(256)S(1)} %bitcast.3), kind=kLoop, calls=%fused_computation | loop fusion | flops 1048576 | bytes 3146752 | tf_op jit(solution)/shard_map/convert_element_type | solution.py:405

commit v5 on v4

--- a/solution.py
+++ b/solution.py
@@ -27,12 +27,11 @@
     sends = [take(halves) for _ in range(ITERS)]
     first = take(halves)
     second = take(halves)
-    mine = take(ITERS)
-    got = take(ITERS)
+    mine, got = take(2)
     relays = take(ITERS * halves - 1)
     late, dense = take(2)
     order, place, cols_ref, rows_ref = take(4)
-    (index_sem, tile_sem, feat_sem, table_sem, send_sem, recv_sem, mass_send, mass_recv, relay_send, relay_recv) = take(10)
+    index_sem, tile_sem, feat_sem, table_sem, send_sem, recv_sem, mass_send, mass_recv, relay_recv = take(9)
 
     nblocks, tile_size = feats[0].shape[0], feats[0].shape[1]
     ntiles = tiles.shape[0]
@@ -57,11 +56,9 @@
     for h in range(halves):
         table_loads[h].start()
     chunk = ntiles // LOADS
-    tile_loads = []
     for k in range(LOADS):
         piece = pl.ds(k * chunk, chunk)
-        tile_loads.append(pltpu.make_async_copy(tiles_hbm.at[piece], tiles.at[piece], tile_sem.at[k]))
-        tile_loads[-1].start()
+        pltpu.make_async_copy(tiles_hbm.at[piece], tiles.at[piece], tile_sem.at[0]).start()
 
     def device_at(distance):
         flat = lax.rem(me + distance + shards, shards)
@@ -121,8 +118,8 @@
         return pltpu.make_async_remote_copy(
             src_ref=sends[it][h].at[pl.ds(o * slots, slots)],
             dst_ref=tables[it][h].at[pl.ds(nblocks + o * slots, slots)],
-            send_sem=send_sem.at[at],
-            recv_sem=recv_sem.at[at],
+            send_sem=send_sem.at[0],
+            recv_sem=recv_sem.at[it * halves + h],
             device_id=peer_at(o),
             device_id_type=MESH,
         )
@@ -139,7 +136,7 @@
         return pltpu.make_async_remote_copy(
             src_ref=sends[it][h].at[pl.ds(passed * slots, slots)],
             dst_ref=relays[at - 1],
-            send_sem=relay_send.at[at - 1],
+            send_sem=send_sem.at[0],
             recv_sem=relay_recv.at[at - 1],
             device_id=device_at(8 * (5 - 2 * passed)),
             device_id_type=MESH,
@@ -151,34 +148,34 @@
         return pltpu.make_async_remote_copy(
             src_ref=relays[at - 1],
             dst_ref=late if at + 1 == len(steps) else table,
-            send_sem=send_sem.at[at * 4 + passed],
-            recv_sem=recv_sem.at[at * 4 + passed],
+            send_sem=send_sem.at[0],
+            recv_sem=recv_sem.at[at + 1 if at + 1 == len(steps) else at],
             device_id=peer_at(direct),
             device_id_type=MESH,
         )
 
     def mass_copy(it, k):
         return pltpu.make_async_remote_copy(
-            src_ref=mine[it],
-            dst_ref=got[it].at[k - 1],
-            send_sem=mass_send.at[it],
+            src_ref=mine.at[it],
+            dst_ref=got.at[it, k - 1],
+            send_sem=mass_send.at[0],
             recv_sem=mass_recv.at[it],
             device_id=device_at(k),
             device_id_type=MESH,
         )
 
-    def mass_all(it):
-        return pltpu.make_async_remote_copy(
-            src_ref=got[it],
-            dst_ref=got[it],
-            send_sem=mass_send.at[it],
-            recv_sem=mass_recv.at[it],
+    def bytes_of(ref, send, recv):
+        return pltpu.make_async_remote_copy(
+            src_ref=ref,
+            dst_ref=ref,
+            send_sem=send,
+            recv_sem=recv,
             device_id=device_at(1),
             device_id_type=MESH,
         )
 
     def mass_first(it, masses):
-        mine[it][...] = jnp.concatenate(masses, axis=1)
+        mine[it] = jnp.concatenate(masses, axis=1)
 
         def one(k, carry):
             mass_copy(it, k).start()
@@ -187,8 +184,8 @@
         lax.fori_loop(1, shards, one, 0, unroll=shards <= UNROLL)
 
     def mass_total(it):
-        mass_all(it).wait_recv()
-        total = mine[it][...] + jnp.sum(got[it][...], axis=0)
+        bytes_of(got.at[it], mass_send.at[0], mass_recv.at[it]).wait_recv()
+        total = mine[it] + jnp.sum(got[it], axis=0)
         return 1.0 / jnp.sqrt(0.05 + total / vertices)
 
     def half_of(gain, h):
@@ -244,7 +241,7 @@
             return mass
 
         none = jnp.zeros((8, LANES), jnp.float32)
-        mass = lax.fori_loop(0, 4, group, none if g2 is None else (none,) * h, unroll=4)
+        mass = lax.fori_loop(0, 4, group, none if g2 is None else (none,) * h, unroll=2)
         return jax.tree.map(lambda part: jnp.sum(part, axis=0, keepdims=True), mass)
 
     def blend_second(h, g1):
@@ -280,17 +277,6 @@
 
         lax.fori_loop(0, nblocks, row, 0)
 
-    def late_wait():
-        at = len(steps) - 1
-        pltpu.make_async_remote_copy(
-            src_ref=late,
-            dst_ref=late,
-            send_sem=send_sem.at[at * 4 + direct],
-            recv_sem=recv_sem.at[at * 4 + direct],
-            device_id=peer_at(direct),
-            device_id_type=MESH,
-        ).wait_recv()
-
     def propagate_late(h, g1, g2):
         right = late[...].reshape(slots * tile_size, LANES)
         count = nblocks // LATE
@@ -316,14 +302,14 @@
             halo_copy(0, h, o).start()
     for h in range(halves):
         table_loads[h].wait()
-    for load in tile_loads:
-        load.wait()
+    pltpu.make_async_copy(tiles_hbm, tiles, tile_sem.at[0]).wait()
     tables[-1][-1][pl.ds(nblocks + direct * slots, slots)] = jnp.zeros(late.shape, jnp.bfloat16)
 
-    def halos(it, h):
-        for o in (0, 1, passed, direct):
-            if o is not direct or (it, h) != steps[-1]:
-                halo_copy(it, h, o).wait_recv()
+    def halos(at):
+        it, h = steps[at]
+        flows = 3 if at + 1 == len(steps) else 4
+        landed = tables[it][h].at[pl.ds(nblocks, flows * slots)]
+        bytes_of(landed, send_sem.at[0], recv_sem.at[at]).wait_recv()
 
     gather_late()
     masses, g1 = [], None
@@ -331,7 +317,7 @@
         if at + 1 < len(steps):
             relay_copy(*steps[at + 1]).wait_recv()
             forward_copy(*steps[at + 1]).start()
-        halos(it, h)
+        halos(at)
         final = h + 1 == halves
         if it == 0:
             masses.append(propagate(0, h))
@@ -342,25 +328,17 @@
         else:
             g2 = mass_total(1)
             masses = list(propagate(2, h, half_of(g1, h), g2))
-            late_wait()
+            bytes_of(late, send_sem.at[0], recv_sem.at[at + 1]).wait_recv()
             masses.append(propagate_late(h, half_of(g1, h), half_of(g2, h)))
         if it == 0 and final:
             mass_first(0, masses)
         if it == 1 and final:
             g1 = mass_total(0)
             mass_first(1, [blend_second(each, half_of(g1, each)) for each in range(halves)])
-    for at, step in enumerate(steps):
-        for o in peers[1:]:
-            halo_copy(*step, o).wait_send()
-        if at:
-            relay_copy(*step).wait_send()
-            forward_copy(*step).wait_send()
-        else:
-            halo_copy(*step, passed).wait_send()
     mass_first(2, masses)
+    bytes_of(tiles.at[pl.ds(0, (5 * len(steps) - 1) * slots)], send_sem.at[0], recv_sem.at[0]).wait_send()
+    bytes_of(got, mass_send.at[0], mass_recv.at[0]).wait_send()
     scale_ref[...] = mass_total(2)
-    for it in range(ITERS):
-        mass_all(it).wait_send()
 
 
 def local(vp_count, rep_count, features, tile_values, tile_cols, halo_rows):
@@ -378,16 +356,14 @@
     scratch += [pltpu.VMEM((nblocks,) + block, bf16)] * (2 * halves)
     scratch += [pltpu.VMEM((4 * slots,) + block, bf16)] * each
     scratch += [pltpu.VMEM((nblocks,) + block, f32)] * (2 * halves)
-    scratch += [pltpu.VMEM((1, classes), f32)] * ITERS
-    scratch += [pltpu.VMEM((shards - 1, 1, classes), f32)] * ITERS
+    scratch += [pltpu.VMEM((ITERS, 1, classes), f32), pltpu.VMEM((ITERS, shards - 1, 1, classes), f32)]
     scratch += [pltpu.VMEM((slots,) + block, bf16)] * each
     scratch += [pltpu.VMEM((nblocks, tile_size, slots * tile_size), bf16)]
     scratch += [pltpu.SMEM((nblocks,), jnp.int32), pltpu.SMEM((nblocks + 4 * slots,), jnp.int32)]
     scratch += [pltpu.SMEM(tile_cols.shape, jnp.int32), pltpu.SMEM(halo_rows.shape, jnp.int32)]
     dma = lambda *shape: pltpu.SemaphoreType.DMA(shape)
-    scratch += [dma(2), dma(LOADS), dma(halves), dma(halves), dma(each * 4), dma(each * 4)]
-    scratch += [dma(ITERS)] * 2
-    scratch += [dma(each - 1)] * 2
+    scratch += [dma(2), dma(1), dma(halves), dma(halves), dma(1), dma(each + 1)]
+    scratch += [dma(1), dma(ITERS), dma(each - 1)]
     operands = (tile_cols, halo_rows, features.reshape(nblocks, tile_size, classes), tile_values)
     finals, scale = pl.pallas_call(
         functools.partial(kernel, vp_count, rep_count, rows * shards, slots, halves),

time: 59 us -> 58.6 us (level)
  no operation moved by 1% of the time
where the time goes in v5:
time: 58.6 us; the launch traced here: 58.5 us
  Pallas kernels  57.3 us (98%)
  other arithmetic  1.18 us (2%)
    pallas_call x1, Pallas kernels, local(): pl.pallas_call(functools.partial(kernel, vp_count, rep_count, rows * shar...  57.3 us
    convert_element_type x1, other arithmetic, local(): return (finals * scale[None]).astype(bf16).reshape(rows, classes)  1.18 us

profile of v5, /device:TPU:0, one launch (start us, length us, event | category | flops | bytes accessed | tf_op | source)
XLA Modules:
  0.0 58.5 jit_solution(4233162198992252463)
XLA Ops:
  0.0 57.3 %shard_map.46 = (f32[16,128,256]{2,1,0:T(8,128)S(1)}, f32[1,256]{1,0:T(1,128)S(1)}) custom-call(s32[256]{0:T(256)} %refs_0_.1, s32[1,4,4]{2,1,0:T(4,128)} %refs_1_.1, bf16[16,128,256]{2,1,0:T(8,128)(2,1)} %bitcast.4, bf16[256,128,128]{2,1,0:T(8,128)(2,1)} %refs_3_.1), custom_call_target="tpu_custom_call" | custom-call | tf_op jit(solution)/shard_map/pallas_call | solution.py:368
  57.3 1.2 %multiply_convert_fusion = bf16[16,128,256]{2,1,0:T(8,128)(2,1)} fusion(f32[16,128,256]{2,1,0:T(8,128)S(1)} %get-tuple-element.7, f32[256]{0:T(256)S(1)} %bitcast.3), kind=kLoop, calls=%fused_computation | loop fusion | flops 1048576 | bytes 3146752 | tf_op jit(solution)/shard_map/convert_element_type | solution.py:381

commit v6 on v5

--- a/solution.py
+++ b/solution.py
@@ -241,7 +241,7 @@
             return mass
 
         none = jnp.zeros((8, LANES), jnp.float32)
-        mass = lax.fori_loop(0, 4, group, none if g2 is None else (none,) * h, unroll=2)
+        mass = lax.fori_loop(0, 4, group, none if g2 is None else (none,) * h, unroll=4 if last else 2)
         return jax.tree.map(lambda part: jnp.sum(part, axis=0, keepdims=True), mass)
 
     def blend_second(h, g1):
@@ -317,8 +317,11 @@
         if at + 1 < len(steps):
             relay_copy(*steps[at + 1]).wait_recv()
             forward_copy(*steps[at + 1]).start()
+        final = h + 1 == halves
+        if it == 1 and final:
+            g1 = mass_total(0)
+            masses = [blend_second(other, half_of(g1, other)) for other in range(h)]
         halos(at)
-        final = h + 1 == halves
         if it == 0:
             masses.append(propagate(0, h))
         elif it == 1:
@@ -333,8 +336,7 @@
         if it == 0 and final:
             mass_first(0, masses)
         if it == 1 and final:
-            g1 = mass_total(0)
-            mass_first(1, [blend_second(each, half_of(g1, each)) for each in range(halves)])
+            mass_first(1, masses + [blend_second(h, half_of(g1, h))])
     mass_first(2, masses)
     bytes_of(tiles.at[pl.ds(0, (5 * len(steps) - 1) * slots)], send_sem.at[0], recv_sem.at[0]).wait_send()
     bytes_of(got, mass_send.at[0], mass_recv.at[0]).wait_send()

time: 58.6 us -> 58.5 us (level)
  no operation moved by 1% of the time
where the time goes in v6:
time: 58.5 us; the launch traced here: 58.3 us
  Pallas kernels  57.1 us (98%)
  other arithmetic  1.18 us (2%)
    pallas_call x1, Pallas kernels, local(): pl.pallas_call(functools.partial(kernel, vp_count, rep_count, rows * shar...  57.1 us
    convert_element_type x1, other arithmetic, local(): return (finals * scale[None]).astype(bf16).reshape(rows, classes)  1.18 us

profile of v6, /device:TPU:0, one launch (start us, length us, event | category | flops | bytes accessed | tf_op | source)
XLA Modules:
  0.0 58.3 jit_solution(8705233960216767986)
XLA Ops:
  0.0 57.1 %shard_map.46 = (f32[16,128,256]{2,1,0:T(8,128)S(1)}, f32[1,256]{1,0:T(1,128)S(1)}) custom-call(s32[256]{0:T(256)} %refs_0_.1, s32[1,4,4]{2,1,0:T(4,128)} %refs_1_.1, bf16[16,128,256]{2,1,0:T(8,128)(2,1)} %bitcast.4, bf16[256,128,128]{2,1,0:T(8,128)(2,1)} %refs_3_.1), custom_call_target="tpu_custom_call" | custom-call | tf_op jit(solution)/shard_map/pallas_call | solution.py:370
  57.1 1.2 %multiply_convert_fusion = bf16[16,128,256]{2,1,0:T(8,128)(2,1)} fusion(f32[16,128,256]{2,1,0:T(8,128)S(1)} %get-tuple-element.7, f32[256]{0:T(256)S(1)} %bitcast.3), kind=kLoop, calls=%fused_computation | loop fusion | flops 1048576 | bytes 3146752 | tf_op jit(solution)/shard_map/convert_element_type | solution.py:383
